TPU v7x, 256 devices: a 4x2x16 block of a 4x16x16 slice. The times are simulated.
256 devices in a mesh: req: 2 (over y), blk: 16 (over z), uly: 8 (over x, core).
Axes of the slice: x: 4, y: 2, z: 16, core: 2. Of those that a mesh axis runs over, the one named last changes fastest.
The devices are a block of a 4x16x16 slice.
Arguments:
- video_qkv: bfloat16 [3, 16384, 3072], P(None, ('req', 'blk', 'uly')), parts along dimension 1, may hold values from -16 to 16
- text_qkv: bfloat16 [3, 512, 3072], P(None, ('req', 'blk', 'uly')), parts along dimension 1, may hold values from -9.5625 to 9.5625
- video_gate: float32 [6144], P('req'), parts along dimension 0, may hold values from 1 to 4
- text_gate: float32 [6144], P('req'), parts along dimension 0, may hold values from 1 to 4
Outputs:
- video_out: bfloat16 [16384, 3072], P(('req', 'blk', 'uly')), parts along dimension 0
- text_out: bfloat16 [512, 3072], P(('req', 'blk', 'uly')), parts along dimension 0
There are 2 independent parts, one for each index of `req`. A program takes and returns all parts, laid end to end along the dimension named above; each array names one. Nothing has to cross between parts.
All inputs are finite; a program needn't handle non-finite values.
Results may differ from a plain program's by a relative error of at most 0.0085.
Values may be sent and summed in bfloat16 or wider, within the bound.
A program may use at most 128 MiB of HBM per device.

v0:
```python
import math

import jax
import jax.numpy as jnp
from jax import lax
from jax.sharding import PartitionSpec as P

HEADS = 24
HD = 128


def merge_block(state, queries, block_pair):
    best, total, summed = state
    scale = 1.0 / math.sqrt(queries.shape[-1])
    scores = (
        jnp.einsum("qhd,khd->hqk", queries, block_pair[0], preferred_element_type=jnp.float32)
        * scale
    )
    new_best = jnp.maximum(best, jnp.max(scores, axis=2))
    factor = jnp.exp(best - new_best)
    raised = jnp.exp(scores - new_best[:, :, None])
    total = total * factor + jnp.sum(raised, axis=2)
    product = jnp.einsum(
        "hqk,khd->hqd",
        raised.astype(jnp.bfloat16),
        block_pair[1],
        preferred_element_type=jnp.float32,
    )
    summed = summed * factor[:, :, None] + product
    return (new_best, total, summed)


def attend(video_heads, text_heads):
    heads = video_heads.shape[3]
    width = video_heads.shape[4]
    rows_video = video_heads.shape[1]
    rows_text = text_heads.shape[1]
    joined = jnp.concatenate((video_heads, text_heads), axis=1)
    rows_all = rows_video + rows_text
    joined = joined.reshape(3, rows_all, heads, width)
    queries = joined[0]
    key_pairs = joined[1:]
    initial = (
        jnp.full((heads, rows_all), -jnp.inf, jnp.float32),
        jnp.zeros((heads, rows_all), jnp.float32),
        jnp.zeros((heads, rows_all, width), jnp.float32),
    )
    piece = lax.all_gather(key_pairs, "blk", axis=1, tiled=True)
    count = piece.shape[1] // rows_all

    def one_block(index, inner):
        block_pair = lax.dynamic_slice_in_dim(piece, index * rows_all, rows_all, 1)
        return merge_block(inner, queries, block_pair)

    best, total, summed = lax.fori_loop(0, count, one_block, initial)
    attended = (summed / total[:, :, None]).transpose(1, 0, 2).astype(jnp.bfloat16)
    video_att = attended[:rows_video].reshape(rows_video, 1, heads, width)
    text_att = attended[rows_video:].reshape(rows_text, 1, heads, width)
    return (video_att, text_att)


def on_device(video_qkv, text_qkv, video_gate, text_gate):
    groups = lax.axis_size("uly")
    local_heads = HEADS // groups
    video_rows = video_qkv.shape[1]
    text_rows = text_qkv.shape[1]
    video_split = video_qkv.reshape(3, video_rows, groups, local_heads, HD)
    text_split = text_qkv.reshape(3, text_rows, groups, local_heads, HD)
    video_heads, text_heads = (
        lax.all_to_all(video_split, "uly", split_axis=2, concat_axis=1, tiled=True),
        lax.all_to_all(text_split, "uly", split_axis=2, concat_axis=1, tiled=True),
    )
    video_att, text_att = attend(video_heads, text_heads)
    video_back, text_back = (
        lax.all_to_all(video_att, "uly", split_axis=0, concat_axis=1, tiled=True),
        lax.all_to_all(text_att, "uly", split_axis=0, concat_axis=1, tiled=True),
    )
    video_flat = video_back.reshape(video_rows, HEADS * HD).astype(jnp.float32)
    text_flat = text_back.reshape(text_rows, HEADS * HD).astype(jnp.float32)
    video_out = (video_flat * video_gate[None, :]).astype(jnp.bfloat16)
    text_out = (text_flat * text_gate[None, :]).astype(jnp.bfloat16)
    return (video_out, text_out)


def solution(mesh):
    in_specs = (
        P(None, ("req", "blk", "uly"), None),
        P(None, ("req", "blk", "uly"), None),
        P("req"),
        P("req"),
    )
    out_specs = (P(("req", "blk", "uly"), None), P(("req", "blk", "uly"), None))
    return jax.shard_map(
        on_device, mesh=mesh, in_specs=in_specs, out_specs=out_specs, check_vma=False
    )
```

profile of v0, /device:TPU:33, one launch (start us, length us, event | category | flops | bytes accessed | tf_op | source)
XLA Modules:
  0.0 317.9 jit_solution(5075370037925039028)
XLA Ops:
  8.6 23.7 %all-to-all-start.1 = ((bf16[3,2,8,3,128]{4,1,3,0,2:T(2,128)(2,1)}), bf16[3,2,8,3,128]{4,1,3,0,2:T(2,128)(2,1)S(1)}, u32[]{:S(2)}, u32[]{:S(2)}) async-start(bf16[3,2,8,3,128]{4,1,3,0,2:T(2,128)(2,1)} %copy.22), calls=%async_computation.1 | async-start | bytes 73728 | tf_op jit(solution)/shard_map/all_to_all | solution.py:71
  32.3 3.2 %reshape.37 = bf16[3,64,8,3,128]{4,3,2,1,0:T(4,128)(2,1)S(1)} reshape(bf16[3,64,3072]{2,1,0:T(8,128)(2,1)} %param.6) | data formatting | bytes 2359296 | tf_op jit(solution)/shard_map/reshape | solution.py:67
  37.1 4.9 %all-to-all-start = ((bf16[3,64,8,3,128]{4,1,3,0,2:T(8,128)(2,1)}), bf16[3,64,8,3,128]{4,1,3,0,2:T(8,128)(2,1)S(1)}, u32[]{:S(2)}, u32[]{:S(2)}) async-start(bf16[3,64,8,3,128]{4,1,3,0,2:T(8,128)(2,1)} %copy.20), calls=%async_computation | async-start | bytes 2359296 | tf_op jit(solution)/shard_map/all_to_all | solution.py:70
  42.0 16.3 %all-to-all-done = bf16[3,64,8,3,128]{4,1,3,0,2:T(8,128)(2,1)S(1)} async-done(((bf16[3,64,8,3,128]{4,1,3,0,2:T(8,128)(2,1)}), bf16[3,64,8,3,128]{4,1,3,0,2:T(8,128)(2,1)S(1)}, u32[]{:S(2)}, u32[]{:S(2)}) %all-to-all-start) | async-done | bytes 1179680 | tf_op jit(solution)/shard_map/all_to_all | solution.py:70
  59.6 144.3 %all-gather.3.cloned.1.call-done = bf16[2,8448,1,3,128]{4,1,3,0,2:T(8,128)(2,1)} async-done(((bf16[2,528,1,3,128]{4,1,3,0,2:T(8,128)(2,1)}), bf16[2,8448,1,3,128]{4,1,3,0,2:T(8,128)(2,1)}) %all-gather.3.cloned.1.call-update) | async-done | bytes 12976144 | tf_op jit(solution)/shard_map/all_gather | solution.py:48
  203.9 79.5 %while.18 = (s32[]{:T(128)}, f32[3,528]{1,0:T(4,128)S(1)}, f32[3,528]{1,0:T(4,128)S(1)}, f32[3,528,128]{2,1,0:T(8,128)S(1)}, bf16[2,8448,3,128]{3,1,2,0:T(8,128)...) while((s32[]{:T(128)}, f32[3,528]{1,0:T(4,128)S(1)}, ...), condition=%wide.region_3.0_spmd.clone, body=%wide.region_0.0_spmd.clone.sunk | while | flops 435519232 | bytes 12976327 | solution.py:55
  206.5 2.3 fusion.31
  211.4 2.3 fusion.31
  216.4 2.3 fusion.31
  221.4 2.3 fusion.31
  226.3 2.3 fusion.31
  231.3 2.3 fusion.31
  236.3 2.3 fusion.31
  241.2 2.3 fusion.31
  246.2 2.3 fusion.31
  251.2 2.3 fusion.31
  261.1 2.3 fusion.31
  266.1 2.3 fusion.31
  271.0 2.3 fusion.31
  281.0 2.3 fusion.31
  286.2 5.1 %all-to-all-start.3 = ((bf16[16,1,3,128]{3,2,1,0:T(4,128)(2,1)}), bf16[16,1,3,128]{3,2,1,0:T(4,128)(2,1)S(1)}, u32[]{:S(2)}, u32[]{:S(2)}) async-start(bf16[16,1,3,128]{3,2,1,0:T(4,128)(2,1)} %slice_bitcast_fusion.1), calls=%async_computation.3 | async-start | bytes 32768 | tf_op jit(solution)/shard_map/all_to_all | solution.py:76
  292.3 3.7 %all-to-all-done.3 = bf16[16,1,3,128]{3,2,1,0:T(4,128)(2,1)S(1)} async-done(((bf16[16,1,3,128]{3,2,1,0:T(4,128)(2,1)}), bf16[16,1,3,128]{3,2,1,0:T(4,128)(2,1)S(1)}, u32[]{:S(2)}, u32[]{:S(2)}) %all-to-all-start.3) | async-done | bytes 12320 | tf_op jit(solution)/shard_map/all_to_all | solution.py:76
  296.0 4.1 %all-to-all-start.2 = ((bf16[512,1,3,128]{3,2,1,0:T(4,128)(2,1)}), bf16[512,1,3,128]{3,2,1,0:T(4,128)(2,1)S(1)}, u32[]{:S(2)}, u32[]{:S(2)}) async-start(bf16[512,1,3,128]{3,2,1,0:T(4,128)(2,1)} %slice_bitcast_fusion), calls=%async_computation.2 | async-start | bytes 1048576 | tf_op jit(solution)/shard_map/all_to_all | solution.py:75
  300.8 8.8 %all-to-all-done.2 = bf16[512,1,3,128]{3,2,1,0:T(4,128)(2,1)S(1)} async-done(((bf16[512,1,3,128]{3,2,1,0:T(4,128)(2,1)}), bf16[512,1,3,128]{3,2,1,0:T(4,128)(2,1)S(1)}, u32[]{:S(2)}, u32[]{:S(2)}) %all-to-all-start.2) | async-done | bytes 393248 | tf_op jit(solution)/shard_map/all_to_all | solution.py:75
  (109 shorter events, 55.9 us)
Async XLA Ops:
  8.6 28.5 %all-to-all-start.1 = ((bf16[3,2,8,3,128]{4,1,3,0,2:T(2,128)(2,1)}), bf16[3,2,8,3,128]{4,1,3,0,2:T(2,128)(2,1)S(1)}, u32[]{:S(2)}, u32[]{:S(2)}) async-start(bf16[3,2,8,3,128]{4,1,3,0,2:T(2,128)(2,1)} %copy.22), calls=%async_computation.1 | async-start | bytes 73728 | tf_op jit(solution)/shard_map/all_to_all | solution.py:71
  37.1 21.2 %all-to-all-start = ((bf16[3,64,8,3,128]{4,1,3,0,2:T(8,128)(2,1)}), bf16[3,64,8,3,128]{4,1,3,0,2:T(8,128)(2,1)S(1)}, u32[]{:S(2)}, u32[]{:S(2)}) async-start(bf16[3,64,8,3,128]{4,1,3,0,2:T(8,128)(2,1)} %copy.20), calls=%async_computation | async-start | bytes 2359296 | tf_op jit(solution)/shard_map/all_to_all | solution.py:70
  42.0 161.9 %all-gather.3.cloned.1.call-start = ((), (), s32[]{:S(2)}) async-start(), calls=%async_computation.4 | async-start | bytes 13787136 | tf_op jit(solution)/shard_map/all_gather | solution.py:48
  283.4 16.8 %copy-start.1 = (f32[3072]{0:T(1024)S(1)}, f32[3072]{0:T(1024)}, u32[]{:S(2)}) copy-start(f32[3072]{0:T(1024)} %param.9) | copy-start | bytes 36868
  283.4 26.9 %copy-start = (f32[3072]{0:T(1024)S(1)}, f32[3072]{0:T(1024)}, u32[]{:S(2)}) copy-start(f32[3072]{0:T(1024)} %param.8) | copy-start | bytes 36868
  286.2 9.8 %all-to-all-start.3 = ((bf16[16,1,3,128]{3,2,1,0:T(4,128)(2,1)}), bf16[16,1,3,128]{3,2,1,0:T(4,128)(2,1)S(1)}, u32[]{:S(2)}, u32[]{:S(2)}) async-start(bf16[16,1,3,128]{3,2,1,0:T(4,128)(2,1)} %slice_bitcast_fusion.1), calls=%async_computation.3 | async-start | bytes 32768 | tf_op jit(solution)/shard_map/all_to_all | solution.py:76
  296.0 13.6 %all-to-all-start.2 = ((bf16[512,1,3,128]{3,2,1,0:T(4,128)(2,1)}), bf16[512,1,3,128]{3,2,1,0:T(4,128)(2,1)S(1)}, u32[]{:S(2)}, u32[]{:S(2)}) async-start(bf16[512,1,3,128]{3,2,1,0:T(4,128)(2,1)} %slice_bitcast_fusion), calls=%async_computation.2 | async-start | bytes 1048576 | tf_op jit(solution)/shard_map/all_to_all | solution.py:75
Sparse Core Ops, SparseCore 0:
  59.6 144.2 all-gather.2
where the time goes:
time: 320 us; the launch traced here: 318 us
  waiting for transfers between devices  173 us (54%)
  matrix products  66.9 us (21%)
  starting transfers between devices  37.8 us (12%)
  other arithmetic  16.5 us (5%)
  between operations  14.2 us (4%)
  local copies, waits for them, and re-layouts  8.66 us (3%)
    all_gather x1, waiting for transfers between devices, attend(): piece = lax.all_gather(key_pairs, 'blk', axis=1, tiled=True)  144 us
    dot_general x16, matrix products, merge_block(): jnp.einsum('hqk,khd->hqd', raised.astype(jnp.bfloat16), block_pair[1], pr...  37.6 us
    dot_general x16, matrix products, merge_block(): jnp.einsum('qhd,khd->hqk', queries, block_pair[0], preferred_element_type...  29.3 us
    all_to_all x1, starting transfers between devices, on_device(): lax.all_to_all(text_split, 'uly', split_axis=2, concat_axis=1, tiled=True)  23.7 us
    all_to_all x1, waiting for transfers between devices, on_device(): lax.all_to_all(video_split, 'uly', split_axis=2, concat_axis=1, tiled=True)  16.3 us
    reduce_sum x16, other arithmetic, merge_block(): total = total * factor + jnp.sum(raised, axis=2)  11.3 us
    all_to_all x1, waiting for transfers between devices, on_device(): lax.all_to_all(video_att, 'uly', split_axis=0, concat_axis=1, tiled=True)  8.77 us
  transfers between devices with their start and end apart: 5, of which 4 were waited for; matrix products, arithmetic and copies ran while one was open for 2% of the time, Pallas kernels for 0%

commit v1 on v0

v1 whole, which is shorter than its diff:
```python
import functools
import math

import jax
import jax.numpy as jnp
from jax import lax
from jax.experimental import pallas as pl
from jax.experimental.pallas import tpu as pltpu
from jax.sharding import PartitionSpec as P

HD = 128
MESH = pl.DeviceIdType.MESH
TILES = 6
PER = 4


def near(j, n):
    return (j + 1) // 2 if j % 2 else (n - j // 2) % n


def tile_sources(nb):
    out = []
    for s in range(TILES):
        if s % 3 == 1:
            first = (s // 3) * PER
            offs = [2 * near(nb // 2 - 1 - first - i, nb // 2) for i in range(PER)]
            out.append((True, offs))
        else:
            first = (s - (s + 1) // 3) * PER
            offs = [near(nb - 1 - first - i, nb) for i in range(PER)]
            out.append((False, offs))
    return out


def kernel(
    nb, nu, vid, txt, vgate, tgate, vout, tout,
    st, stt, kvb, txb, qb, qtb, ob, otb, qf, qq, ktx, tf, m_sc, acc_sc,
    l_st, l_kv, l_q, zs_kv, zr_kv, zs_t, zr_t, zs_q, zr_q, zs_qt, zr_qt,
    xs, xl, xr, xf0, xf1, pc, ts, tr, os_, orv, ots, otr, ol,
):
    z = lax.axis_index("blk")
    u = lax.axis_index("uly")
    rows = vid.shape[1]
    trows = txt.shape[1]
    up = u + 1 - 2 * lax.rem(u, 2)
    ul = lax.rem(u + nu - 2, nu)
    ur = lax.rem(u + 2, nu)
    uf = lax.rem(u + 4, nu)

    barrier = pltpu.get_barrier_semaphore()
    for e in range(1, nb):
        pl.semaphore_signal(
            barrier, inc=1, device_id={"blk": lax.rem(z + e, nb)}, device_id_type=MESH
        )
    for e in range(1, nu):
        pl.semaphore_signal(
            barrier, inc=1, device_id={"uly": lax.rem(u + e, nu)}, device_id_type=MESH
        )

    def cols(h):
        return pl.ds(pl.multiple_of(h * HD, HD), HD)

    heads = st.shape[0]

    def stage(h, _):
        pltpu.make_async_copy(vid.at[:, :, cols(h)], st.at[h], l_st.at[0]).start()
        pltpu.make_async_copy(txt.at[:, :, cols(h)], stt.at[h], l_st.at[1]).start()
        return 0

    lax.fori_loop(0, heads, stage, 0)

    def low(t):
        return 3 * (t // 2) + lax.rem(t, 2)

    def own(t):
        return 3 * (t // 2) + 2 * lax.rem(t, 2)

    def shared(t):
        return 3 * (t // 2) + 1

    hs = low(z)
    for k in range(2):
        pltpu.make_async_copy(
            vid.at[pl.ds(1, 2), :, cols(hs + k)], kvb.at[u, 0, k], l_kv.at[k]
        ).start()
        pltpu.make_async_copy(
            txt.at[pl.ds(1, 2), :, cols(hs + k)], txb.at[u, 0, k], l_kv.at[2 + k]
        ).start()
    plan = tile_sources(nb)
    locals_q = []
    for s, (both, offs) in enumerate(plan):
        for i, d in enumerate(offs):
            if d == 0:
                h = shared(z) if both else own(z)
                a = pltpu.make_async_copy(vid.at[0, :, cols(h)], qb.at[s, i], l_q.at[2 * len(locals_q)])
                b = pltpu.make_async_copy(txt.at[0, :, cols(h)], qtb.at[s, i], l_q.at[2 * len(locals_q) + 1])
                a.start()
                b.start()
                locals_q.append((a, b))

    pltpu.make_async_copy(st, st, l_st.at[0]).wait()
    pltpu.make_async_copy(stt, stt, l_st.at[1]).wait()
    pl.semaphore_wait(barrier, nb - 1 + nu - 1)

    def send(src, dst, ss, rs, dev):
        pltpu.make_async_remote_copy(
            src_ref=src, dst_ref=dst, send_sem=ss, recv_sem=rs, device_id=dev, device_id_type=MESH
        ).start()

    for j in range(1, nb):
        d = near(j, nb)
        t = lax.rem(z + nb - d, nb)
        h = low(t)
        send(st.at[pl.ds(h, 2), pl.ds(1, 2)], kvb.at[u, d], zs_kv, zr_kv.at[d], {"blk": t})
        send(stt.at[pl.ds(h, 2), pl.ds(1, 2)], txb.at[u, d], zs_t, zr_t, {"blk": t})
    for s, (both, offs) in enumerate(plan):
        for i, d in enumerate(offs):
            if d == 0:
                continue
            t = lax.rem(z + nb - d, nb)
            h = shared(t) if both else own(t)
            send(st.at[h, 0], qb.at[s, i], zs_q, zr_q.at[s], {"blk": t})
            send(stt.at[h, 0], qtb.at[s, i], zs_qt, zr_qt.at[s], {"blk": t})

    def arrived(ref, sem):
        pltpu.make_async_copy(ref, ref, sem).wait()

    right, left, partner = {"uly": ur}, {"uly": ul}, {"uly": up}

    def own_piece(d):
        if d == 0:
            for k in range(2):
                arrived(kvb.at[u, 0, k], l_kv.at[k])
        else:
            arrived(kvb.at[u, d], zr_kv.at[d])
        piece = kvb.at[u, d]
        send(piece, piece, xs.at[0], xl.at[d], right)
        send(piece, piece, xs.at[1], xr.at[d], left)
        send(piece, piece, xs.at[2], pc, partner)

    def next_piece(d):
        arrived(kvb.at[ul, d], xl.at[d])
        send(kvb.at[ul, d, 0], kvb.at[ul, d, 0], xs.at[0], xf0.at[d], right)
        send(kvb.at[ul, d], kvb.at[ul, d], xs.at[2], pc, partner)
        arrived(kvb.at[ur, d], xr.at[d])
        send(kvb.at[ur, d, 1], kvb.at[ur, d, 1], xs.at[1], xf1.at[d], left)
        send(kvb.at[ur, d], kvb.at[ur, d], xs.at[2], pc, partner)

    def far_piece(d):
        arrived(kvb.at[uf, d, 0], xf0.at[d])
        send(kvb.at[uf, d, 0], kvb.at[uf, d, 0], xs.at[2], pc, partner)
        arrived(kvb.at[uf, d, 1], xf1.at[d])
        send(kvb.at[uf, d, 1], kvb.at[uf, d, 1], xs.at[2], pc, partner)

    for j in range(nb + 2):
        if j < nb:
            own_piece(near(j, nb))
        if j == nb - 1:
            for k in range(2):
                arrived(txb.at[u, 0, k], l_kv.at[2 + k])
            arrived(txb.at[u, pl.ds(1, nb - 1)], zr_t)
            for e in range(1, nu):
                send(txb.at[u], txb.at[u], ts, tr, {"uly": lax.rem(u + e, nu)})
        if 1 <= j <= nb:
            next_piece(near(j - 1, nb))
        if j >= 2:
            far_piece(near(j - 2, nb))
    arrived(txb.at[pl.ds(0, nu - 1)], tr)

    for k in range(2):
        for kv in range(2):
            for v in range(nu):
                for d in range(nb):
                    at = (v * nb + d) * trows
                    tf[at : at + trows, :] = txb[v, d, k, kv].astype(jnp.float32)
            ktx[k, kv] = tf[...].astype(jnp.bfloat16)
    arrived(kvb.at[pl.ds(0, nu // 2)], pc)

    scale = math.log2(math.e) / math.sqrt(HD)
    vrows = PER * rows
    par = lax.rem(z, 2)

    def update(keys, values):
        kk = jnp.concatenate((keys, keys), axis=1)
        scores = lax.dot_general(
            qq[...], kk, (((1,), (1,)), ((), ())), preferred_element_type=jnp.float32
        )
        old = m_sc[...]
        best = jnp.maximum(old, jnp.max(scores, axis=1, keepdims=True))
        m_sc[...] = best
        raised = jnp.exp2(scores - best[:, :1]).astype(jnp.bfloat16)
        factor = jnp.exp2(old - best)
        vv = jnp.concatenate((values, jnp.ones_like(values)), axis=1)
        product = jnp.dot(raised, vv, preferred_element_type=jnp.float32)
        acc_sc[:, :HD] = acc_sc[:, :HD] * factor + product[:, :HD]
        acc_sc[:, HD:] = acc_sc[:, HD:] * factor + product[:, HD:]

    count = 0
    for s, (both, offs) in enumerate(plan):
        remote = sum(d != 0 for d in offs)
        if remote < PER:
            a, b = locals_q[count]
            a.wait()
            b.wait()
            count += 1
        arrived(qb.at[s, pl.ds(0, remote)], zr_q.at[s])
        arrived(qtb.at[s, pl.ds(0, remote)], zr_qt.at[s])
        qf[0:vrows, :] = qb[s].astype(jnp.float32).reshape(vrows, HD)
        for i in range(PER):
            at = vrows + i * trows
            qf[at : at + trows, :] = qtb[s, i].astype(jnp.float32)
        scaled = qf[...] * scale
        high = scaled.astype(jnp.bfloat16)
        qq[:, :HD] = high
        qq[:, HD:] = (scaled - high.astype(jnp.float32)).astype(jnp.bfloat16)
        m_sc[...] = jnp.full(m_sc.shape, -jnp.inf, jnp.float32)
        acc_sc[...] = jnp.zeros(acc_sc.shape, jnp.float32)
        slot = par if not both else 1 - par

        def chunk(c, _):
            update(
                kvb[c, :, slot, 0].reshape(nb * rows, HD),
                kvb[c, :, slot, 1].reshape(nb * rows, HD),
            )
            return 0

        lax.fori_loop(0, nu, chunk, 0)
        update(ktx[slot, 0], ktx[slot, 1])

        h = shared(z) if both else own(z)
        attended = (acc_sc[:, :HD] / acc_sc[:, HD:]).astype(jnp.bfloat16).astype(jnp.float32)
        gated = attended[:vrows] * vgate[pl.ds(h, 1), :]
        ob[s] = gated.astype(jnp.bfloat16).reshape(PER, rows, HD)
        tgated = attended[vrows:] * tgate[pl.ds(h, 1), :]
        for i in range(PER):
            otb[s, i] = tgated[i * trows : (i + 1) * trows].astype(jnp.bfloat16)
        for i, d in enumerate(offs):
            if d == 0:
                pltpu.make_async_copy(ob.at[s, i], vout.at[:, cols(h)], ol.at[2 * (count - 1)]).start()
                pltpu.make_async_copy(otb.at[s, i], tout.at[:, cols(h)], ol.at[2 * (count - 1) + 1]).start()
            else:
                t = lax.rem(z + d, nb)
                send(ob.at[s, i], vout.at[:, cols(h)], os_, orv, {"blk": t})
                send(otb.at[s, i], tout.at[:, cols(h)], ots, otr, {"blk": t})

    for k in range(2):
        arrived(ob.at[0, 0], ol.at[2 * k])
        arrived(otb.at[0, 0], ol.at[2 * k + 1])
    n_out = nb - 1 + nb // 2 - 1
    some = kvb.at[0, pl.ds(0, n_out // 2), 0]
    small = txb.at[0, pl.ds(0, n_out // 2), 0]
    for sem in (os_, orv, zs_q):
        arrived(some, sem)
    for sem in (ots, otr, zs_qt):
        arrived(small, sem)
    arrived(kvb.at[0, pl.ds(0, nb - 1)], zs_kv)
    arrived(txb.at[0, pl.ds(0, nb - 1)], zs_t)
    arrived(kvb.at[pl.ds(0, 3), pl.ds(0, nb // 2)], xs.at[0])
    arrived(kvb.at[pl.ds(0, 3), pl.ds(0, nb // 2)], xs.at[1])
    arrived(kvb.at[pl.ds(0, nu // 2)], xs.at[2])
    arrived(txb.at[pl.ds(0, nu - 1)], ts)


def on_device(video_qkv, text_qkv, video_gate, text_gate):
    nb = lax.axis_size("blk")
    nu = lax.axis_size("uly")
    rows, width = video_qkv.shape[1:]
    trows = text_qkv.shape[1]
    heads = width // HD
    bf, f32 = jnp.bfloat16, jnp.float32
    tile = PER * (rows + trows)
    dma = pltpu.SemaphoreType.DMA
    hbm = pl.BlockSpec(memory_space=pl.ANY)
    vmem = pl.BlockSpec(memory_space=pltpu.VMEM)
    return pl.pallas_call(
        functools.partial(kernel, nb, nu),
        out_shape=(
            jax.ShapeDtypeStruct((rows, width), bf),
            jax.ShapeDtypeStruct((trows, width), bf),
        ),
        in_specs=[hbm, hbm, vmem, vmem],
        out_specs=(hbm, hbm),
        scratch_shapes=[
            pltpu.VMEM((heads, 3, rows, HD), bf),
            pltpu.VMEM((heads, 3, trows, HD), bf),
            pltpu.VMEM((nu, nb, 2, 2, rows, HD), bf),
            pltpu.VMEM((nu, nb, 2, 2, trows, HD), bf),
            pltpu.VMEM((TILES, PER, rows, HD), bf),
            pltpu.VMEM((TILES, PER, trows, HD), bf),
            pltpu.VMEM((TILES, PER, rows, HD), bf),
            pltpu.VMEM((TILES, PER, trows, HD), bf),
            pltpu.VMEM((tile, HD), f32),
            pltpu.VMEM((tile, 2 * HD), bf),
            pltpu.VMEM((2, 2, nu * nb * trows, HD), bf),
            pltpu.VMEM((nu * nb * trows, HD), f32),
            pltpu.VMEM((tile, HD), f32),
            pltpu.VMEM((tile, 2 * HD), f32),
            dma((2,)), dma((4,)), dma((4,)),
            dma(()), dma((nb,)), dma(()), dma(()), dma(()), dma((TILES,)), dma(()), dma((TILES,)),
            dma((3,)), dma((nb,)), dma((nb,)), dma((nb,)), dma((nb,)), dma(()),
            dma(()), dma(()),
            dma(()), dma(()), dma(()), dma(()), dma((4,)),
        ],
        compiler_params=pltpu.CompilerParams(
            collective_id=0, has_side_effects=True, vmem_limit_bytes=60 * 1024 * 1024
        ),
        name="joint_attention",
    )(video_qkv, text_qkv, video_gate.reshape(heads, HD), text_gate.reshape(heads, HD))


def solution(mesh):
    in_specs = (
        P(None, ("req", "blk", "uly"), None),
        P(None, ("req", "blk", "uly"), None),
        P("req"),
        P("req"),
    )
    out_specs = (P(("req", "blk", "uly"), None), P(("req", "blk", "uly"), None))
    return jax.shard_map(
        on_device, mesh=mesh, in_specs=in_specs, out_specs=out_specs, check_vma=False
    )
```

time: 320 us -> 160 us (0.50)
  waiting for transfers between devices: 173 us -> 0 us
  Pallas kernels: 0 us -> 156 us
  matrix products: 66.9 us -> 0 us
  starting transfers between devices: 37.8 us -> 0 us
  other arithmetic: 16.5 us -> 0 us
  between operations: 14.2 us -> 0.64 us
  local copies, waits for them, and re-layouts: 8.66 us -> 3.08 us
    pallas_call x0 -> x1, Pallas kernels: none -> 156 us  [on_device(): pl.pallas_call(functools.partial(kernel, nb, nu), out_shape=(jax.ShapeDty...]
    all_gather x1 -> x0, waiting for transfers between devices: 144 us -> none  [attend(): piece = lax.all_gather(key_pairs, 'blk', axis=1, tiled=True)]
    dot_general x32 -> x0, matrix products: 66.9 us -> none  [the longest x16 37.6 us: merge_block(): jnp.einsum('hqk,khd->hqd', raised.astype(jnp.bfloat16), block_pair[1], pr...]
    all_to_all x4 -> x0, starting transfers between devices: 37.8 us -> none  [the longest x1 23.7 us: on_device(): lax.all_to_all(text_split, 'uly', split_axis=2, concat_axis=1, tiled=True)]
    all_to_all x4 -> x0, waiting for transfers between devices: 28.8 us -> none  [the longest x1 16.3 us: on_device(): lax.all_to_all(video_split, 'uly', split_axis=2, concat_axis=1, tiled=True)]
    reduce_sum x16 -> x0, other arithmetic: 11.3 us -> none  [merge_block(): total = total * factor + jnp.sum(raised, axis=2)]
    reshape x6 -> x0, local copies, waits for them, and re-layouts: 7.86 us -> none  [the longest x2 4.81 us: on_device(): video_split = video_qkv.reshape(3, video_rows, groups, local_heads, HD)]
    convert_element_type x5 -> x0, other arithmetic: 3.71 us -> none  [the longest x1 2.05 us: attend(): (summed / total[:, :, None]).transpose(1, 0, 2).astype(jnp.bfloat16)]
  transfers between devices with their start and end apart: 5 -> 0, of which waited for: 4 -> 0; matrix products, arithmetic and copies ran while one was open for 2% -> 0% of each run, Pallas kernels for 0% -> 0%
where the time goes in v1:
time: 160 us; the launch traced here: 159 us
  Pallas kernels  156 us (98%)
  local copies, waits for them, and re-layouts  3.08 us (2%)
    pallas_call x1, Pallas kernels, on_device(): pl.pallas_call(functools.partial(kernel, nb, nu), out_shape=(jax.ShapeDty...  156 us

profile of v1, /device:TPU:33, one launch (start us, length us, event | category | flops | bytes accessed | tf_op | source)
XLA Modules:
  0.0 159.4 jit_solution(10463595825060476837)
XLA Ops:
  0.6 155.7 %joint_attention.1 = (bf16[64,3072]{1,0:T(8,128)(2,1)}, bf16[2,3072]{1,0:T(2,128)(2,1)}) custom-call(bf16[3,64,3072]{2,1,0:T(8,128)(2,1)} %vid.1, bf16[3,2,3072]{2,1,0:T(2,128)(2,1)} %txt.1, f32[24,128]{1,0:T(8,128)} %bitcast.2, f32[24,128]{1,0:T(8,128)} %bitcast.3), custom_call_target="tpu_custom_call" | custom-call | tf_op jit(solution)/shard_map/joint_attention/pallas_call | solution.py:275
  156.3 1.8 %copy.8 = bf16[64,3072]{1,0:T(8,128)(2,1)} copy(bf16[64,3072]{1,0:T(8,128)(2,1)} %get-tuple-element.4) | data formatting | bytes 786432
  158.1 1.3 copy.9

commit v2 on v1

v2 whole, which is shorter than its diff:
```python
import functools
import math

import jax
import jax.numpy as jnp
from jax import lax
from jax.experimental import pallas as pl
from jax.experimental.pallas import tpu as pltpu
from jax.sharding import PartitionSpec as P

HD = 128
MESH = pl.DeviceIdType.MESH
TILES = 3
LAG = 3


def near(j, n):
    if isinstance(j, int):
        return (j + 1) // 2 if j % 2 else (n - j // 2) % n
    return jnp.where(lax.rem(j, 2) == 1, (j + 1) // 2, lax.rem(n - j // 2, n))


def kernel(
    nb, nu, vid, txt, vgate, tgate, vout, tout,
    st, stt, kvb, txb, qb, qtb, ob, otb, qf, qq, ktx, tf, m_sc, acc_sc, s_a, s_b,
    l_st, l_kv, l_q, zs_kv, zr_kv, zs_t, zr_t, zs_q, zr_q, zs_qt, zr_qt,
    xs, xl, xr, xf0, xf1, pc, ts, tr, os_, orv, ots, otr, ol,
):
    z = lax.axis_index("blk")
    u = lax.axis_index("uly")
    rows = vid.shape[1]
    trows = txt.shape[1]
    per = nb // 2
    up = u + 1 - 2 * lax.rem(u, 2)
    ul = lax.rem(u + nu - 2, nu)
    ur = lax.rem(u + 2, nu)
    uf = lax.rem(u + 4, nu)
    par = lax.rem(z, 2)

    barrier = pltpu.get_barrier_semaphore()
    for e in range(1, nb):
        pl.semaphore_signal(
            barrier, inc=1, device_id={"blk": lax.rem(z + e, nb)}, device_id_type=MESH
        )
    for e in range(1, nu):
        pl.semaphore_signal(
            barrier, inc=1, device_id={"uly": lax.rem(u + e, nu)}, device_id_type=MESH
        )

    def cols(h):
        return pl.ds(pl.multiple_of(h * HD, HD), HD)

    heads = st.shape[0]

    def stage(h, _):
        pltpu.make_async_copy(vid.at[:, :, cols(h)], st.at[h], l_st.at[0]).start()
        pltpu.make_async_copy(txt.at[:, :, cols(h)], stt.at[h], l_st.at[1]).start()
        return 0

    lax.fori_loop(0, heads, stage, 0)

    def low(t):
        return 3 * (t // 2) + lax.rem(t, 2)

    def own(t):
        return 3 * (t // 2) + 2 * lax.rem(t, 2)

    def shared(t):
        return 3 * (t // 2) + 1

    def shared_to(e):
        up_to = lax.rem(z + e, nb)
        return jnp.where(lax.rem(up_to, 2) == 0, up_to, lax.rem(z + nb - e, nb))

    def shared_back(e):
        return lax.rem(z + nb + (2 * par - 1) * e, nb)

    hs = low(z)
    for k in range(2):
        pltpu.make_async_copy(
            vid.at[pl.ds(1, 2), :, cols(hs + k)], kvb.at[u, 0, k], l_kv.at[k]
        ).start()
        pltpu.make_async_copy(
            txt.at[pl.ds(1, 2), :, cols(hs + k)], txb.at[u, 0, k], l_kv.at[2 + k]
        ).start()
    for k, (s, h) in enumerate(((1, own(z)), (2, shared(z)))):
        pltpu.make_async_copy(vid.at[0, :, cols(h)], qb.at[s, per - 1], l_q.at[2 * k]).start()
        pltpu.make_async_copy(txt.at[0, :, cols(h)], qtb.at[s, per - 1], l_q.at[2 * k + 1]).start()

    pltpu.make_async_copy(st, st, l_st.at[0]).wait()
    pltpu.make_async_copy(stt, stt, l_st.at[1]).wait()
    pl.semaphore_wait(barrier, nb - 1 + nu - 1)

    def send(src, dst, ss, rs, dev):
        pltpu.make_async_remote_copy(
            src_ref=src, dst_ref=dst, send_sem=ss, recv_sem=rs, device_id=dev, device_id_type=MESH
        ).start()

    for s in range(TILES):
        for i in range(per):
            if s < 2:
                d = near(nb - 1 - per * s - i, nb)
                t = lax.rem(z + nb - d, nb)
                h = own(t)
            else:
                d = per - 1 - i
                t = shared_to(d)
                h = shared(t)
            if d != 0:
                send(st.at[h, 0], qb.at[s, i], zs_q, zr_q.at[s], {"blk": t})
                send(stt.at[h, 0], qtb.at[s, i], zs_qt, zr_qt.at[s], {"blk": t})
    for j in range(1, nb):
        d = near(j, nb)
        t = lax.rem(z + nb - d, nb)
        h = low(t)
        send(stt.at[pl.ds(h, 2), pl.ds(1, 2)], txb.at[u, d], zs_t, zr_t, {"blk": t})
    for j in range(1, nb):
        d = near(j, nb)
        t = lax.rem(z + nb - d, nb)
        h = low(t)
        send(st.at[pl.ds(h, 2), pl.ds(1, 2)], kvb.at[u, d], zs_kv, zr_kv.at[d], {"blk": t})

    def arrived(ref, sem):
        pltpu.make_async_copy(ref, ref, sem).wait()

    right, left, partner = {"uly": ur}, {"uly": ul}, {"uly": up}

    def pass_own(d):
        piece = kvb.at[u, d]
        send(piece, piece, xs.at[0], xl.at[d], right)
        send(piece, piece, xs.at[1], xr.at[d], left)
        send(piece, piece, xs.at[2], pc.at[d], partner)

    def own_piece(d):
        arrived(kvb.at[u, d], zr_kv.at[d])
        pass_own(d)

    def next_piece(d):
        arrived(kvb.at[ul, d], xl.at[d])
        send(kvb.at[ul, d, 0], kvb.at[ul, d, 0], xs.at[0], xf0.at[d], right)
        send(kvb.at[ul, d], kvb.at[ul, d], xs.at[2], pc.at[d], partner)
        arrived(kvb.at[ur, d], xr.at[d])
        send(kvb.at[ur, d, 1], kvb.at[ur, d, 1], xs.at[1], xf1.at[d], left)
        send(kvb.at[ur, d], kvb.at[ur, d], xs.at[2], pc.at[d], partner)

    def far_piece(d):
        arrived(kvb.at[uf, d, 0], xf0.at[d])
        send(kvb.at[uf, d, 0], kvb.at[uf, d, 0], xs.at[2], pc.at[d], partner)
        arrived(kvb.at[uf, d, 1], xf1.at[d])
        send(kvb.at[uf, d, 1], kvb.at[uf, d, 1], xs.at[2], pc.at[d], partner)

    scale = math.log2(math.e) / math.sqrt(HD)
    vrows = per * rows
    n_all = vrows + per * trows
    slots = (par, par, 1 - par)

    def scores_of(s, keys):
        kk = jnp.concatenate((keys, keys), axis=1)
        return lax.dot_general(
            qq[s], kk, (((1,), (1,)), ((), ())), preferred_element_type=jnp.float32
        )

    def soften(s, sref, values):
        scores = sref[...]
        old = m_sc[s]
        best = jnp.maximum(old, jnp.max(scores, axis=1, keepdims=True))
        m_sc[s] = best
        raised = jnp.exp2(scores - best[:, :1]).astype(jnp.bfloat16)
        factor = jnp.exp2(old - best)
        vv = jnp.concatenate((values, jnp.ones_like(values)), axis=1)
        product = jnp.dot(raised, vv, preferred_element_type=jnp.float32)
        acc_sc[s, :, :HD] = acc_sc[s, :, :HD] * factor + product[:, :HD]
        acc_sc[s, :, HD:] = acc_sc[s, :, HD:] * factor + product[:, HD:]

    def step(block, n):
        bufs = (s_a, s_b)
        for s in range(TILES + 1):
            if s < TILES:
                bufs[s % 2][:, :n] = scores_of(s, block(slots[s], 0))
            if s > 0:
                soften(s - 1, bufs[(s - 1) % 2].at[:, :n], block(slots[s - 1], 1))

    for k in range(2):
        arrived(kvb.at[u, 0, k], l_kv.at[k])
    pass_own(0)
    for j in range(1, LAG):
        own_piece(near(j, nb))
        next_piece(near(j - 1, nb))
        if j >= 2:
            far_piece(near(j - 2, nb))

    for k in range(2):
        arrived(txb.at[u, 0, k], l_kv.at[2 + k])
    arrived(txb.at[u, pl.ds(1, nb - 1)], zr_t)
    for e in range(1, nu):
        send(txb.at[u], txb.at[u], ts, tr, {"uly": lax.rem(u + e, nu)})

    for s in range(TILES):
        remote = per
        if s > 0:
            arrived(qb.at[s, per - 1], l_q.at[2 * (s - 1)])
            arrived(qtb.at[s, per - 1], l_q.at[2 * (s - 1) + 1])
            remote = per - 1
        arrived(qb.at[s, pl.ds(0, remote)], zr_q.at[s])
        arrived(qtb.at[s, pl.ds(0, remote)], zr_qt.at[s])
        qf[0:vrows, :] = qb[s].astype(jnp.float32).reshape(vrows, HD)
        for i in range(per):
            at = vrows + i * trows
            qf[at : at + trows, :] = qtb[s, i].astype(jnp.float32)
        scaled = qf[...] * scale
        high = scaled.astype(jnp.bfloat16)
        qq[s, :, :HD] = high
        qq[s, :, HD:] = (scaled - high.astype(jnp.float32)).astype(jnp.bfloat16)
    m_sc[...] = jnp.full(m_sc.shape, -jnp.inf, jnp.float32)
    acc_sc[...] = jnp.zeros(acc_sc.shape, jnp.float32)

    arrived(txb.at[pl.ds(0, nu - 1)], tr)
    for k in range(2):
        for kv in range(2):
            for v in range(nu):
                for d in range(nb):
                    at = (v * nb + d) * trows
                    tf[at : at + trows, :] = txb[v, d, k, kv].astype(jnp.float32)
            ktx[k, kv] = tf[...].astype(jnp.bfloat16)
    step(lambda slot, kv: ktx[slot, kv], nu * nb * trows)

    def turn(j, _):
        @pl.when(j < nb)
        def _():
            own_piece(near(j, nb))

        @pl.when(j < nb + 1)
        def _():
            next_piece(near(j - 1, nb))

        @pl.when(j < nb + 2)
        def _():
            far_piece(near(j - 2, nb))

        d = near(j - LAG, nb)
        arrived(kvb.at[pl.ds(0, nu // 2), 0], pc.at[d])
        step(lambda slot, kv: kvb[:, d, slot, kv].reshape(nu * rows, HD), nu * rows)
        return 0

    lax.fori_loop(LAG, nb + LAG, turn, 0)

    for s in range(TILES):
        h = own(z) if s < 2 else shared(z)
        attended = (acc_sc[s, :, :HD] / acc_sc[s, :, HD:]).astype(jnp.bfloat16).astype(jnp.float32)
        gated = attended[:vrows] * vgate[pl.ds(h, 1), :]
        ob[s] = gated.astype(jnp.bfloat16).reshape(per, rows, HD)
        tgated = attended[vrows:] * tgate[pl.ds(h, 1), :]
        for i in range(per):
            otb[s, i] = tgated[i * trows : (i + 1) * trows].astype(jnp.bfloat16)
        for i in range(per):
            if s < 2:
                d = near(nb - 1 - per * s - i, nb)
                t = lax.rem(z + d, nb)
            else:
                d = per - 1 - i
                t = shared_back(d)
            if d == 0:
                at = 2 * (s - 1)
                pltpu.make_async_copy(ob.at[s, i], vout.at[:, cols(h)], ol.at[at]).start()
                pltpu.make_async_copy(otb.at[s, i], tout.at[:, cols(h)], ol.at[at + 1]).start()
            else:
                send(ob.at[s, i], vout.at[:, cols(h)], os_, orv, {"blk": t})
                send(otb.at[s, i], tout.at[:, cols(h)], ots, otr, {"blk": t})

    for k in range(2):
        arrived(ob.at[0, 0], ol.at[2 * k])
        arrived(otb.at[0, 0], ol.at[2 * k + 1])
    n_out = nb - 1 + per - 1
    some = kvb.at[0, pl.ds(0, n_out // 2), 0]
    small = txb.at[0, pl.ds(0, n_out // 2), 0]
    for sem in (os_, orv, zs_q):
        arrived(some, sem)
    for sem in (ots, otr, zs_qt):
        arrived(small, sem)
    arrived(kvb.at[0, pl.ds(0, nb - 1)], zs_kv)
    arrived(txb.at[0, pl.ds(0, nb - 1)], zs_t)
    arrived(kvb.at[pl.ds(0, 3), pl.ds(0, nb // 2)], xs.at[0])
    arrived(kvb.at[pl.ds(0, 3), pl.ds(0, nb // 2)], xs.at[1])
    arrived(kvb.at[pl.ds(0, nu // 2)], xs.at[2])
    arrived(txb.at[pl.ds(0, nu - 1)], ts)


def on_device(video_qkv, text_qkv, video_gate, text_gate):
    nb = lax.axis_size("blk")
    nu = lax.axis_size("uly")
    rows, width = video_qkv.shape[1:]
    trows = text_qkv.shape[1]
    heads = width // HD
    bf, f32 = jnp.bfloat16, jnp.float32
    per = nb // 2
    tile = per * (rows + trows)
    dma = pltpu.SemaphoreType.DMA
    hbm = pl.BlockSpec(memory_space=pl.ANY)
    vmem = pl.BlockSpec(memory_space=pltpu.VMEM)
    return pl.pallas_call(
        functools.partial(kernel, nb, nu),
        out_shape=(
            jax.ShapeDtypeStruct((rows, width), bf),
            jax.ShapeDtypeStruct((trows, width), bf),
        ),
        in_specs=[hbm, hbm, vmem, vmem],
        out_specs=(hbm, hbm),
        scratch_shapes=[
            pltpu.VMEM((heads, 3, rows, HD), bf),
            pltpu.VMEM((heads, 3, trows, HD), bf),
            pltpu.VMEM((nu, nb, 2, 2, rows, HD), bf),
            pltpu.VMEM((nu, nb, 2, 2, trows, HD), bf),
            pltpu.VMEM((TILES, per, rows, HD), bf),
            pltpu.VMEM((TILES, per, trows, HD), bf),
            pltpu.VMEM((TILES, per, rows, HD), bf),
            pltpu.VMEM((TILES, per, trows, HD), bf),
            pltpu.VMEM((tile, HD), f32),
            pltpu.VMEM((TILES, tile, 2 * HD), bf),
            pltpu.VMEM((2, 2, nu * nb * trows, HD), bf),
            pltpu.VMEM((nu * nb * trows, HD), f32),
            pltpu.VMEM((TILES, tile, HD), f32),
            pltpu.VMEM((TILES, tile, 2 * HD), f32),
            pltpu.VMEM((tile, nu * rows), f32),
            pltpu.VMEM((tile, nu * rows), f32),
            dma((2,)), dma((4,)), dma((4,)),
            dma(()), dma((nb,)), dma(()), dma(()), dma(()), dma((TILES,)), dma(()), dma((TILES,)),
            dma((3,)), dma((nb,)), dma((nb,)), dma((nb,)), dma((nb,)), dma((nb,)),
            dma(()), dma(()),
            dma(()), dma(()), dma(()), dma(()), dma((4,)),
        ],
        compiler_params=pltpu.CompilerParams(
            collective_id=0, has_side_effects=True, vmem_limit_bytes=60 * 1024 * 1024
        ),
        name="joint_attention",
    )(video_qkv, text_qkv, video_gate.reshape(heads, HD), text_gate.reshape(heads, HD))


def solution(mesh):
    in_specs = (
        P(None, ("req", "blk", "uly"), None),
        P(None, ("req", "blk", "uly"), None),
        P("req"),
        P("req"),
    )
    out_specs = (P(("req", "blk", "uly"), None), P(("req", "blk", "uly"), None))
    return jax.shard_map(
        on_device, mesh=mesh, in_specs=in_specs, out_specs=out_specs, check_vma=False
    )
```

time: 160 us -> 138 us (0.86)
  Pallas kernels: 156 us -> 134 us
    pallas_call x1, Pallas kernels: 156 us -> 134 us  [on_device(): pl.pallas_call(functools.partial(kernel, nb, nu), out_shape=(jax.ShapeDty...]
where the time goes in v2:
time: 138 us
  Pallas kernels  134 us (97%)
  local copies, waits for them, and re-layouts  3.08 us (2%)
    pallas_call x1, Pallas kernels, on_device(): pl.pallas_call(functools.partial(kernel, nb, nu), out_shape=(jax.ShapeDty...  134 us
    unnamed x2, local copies, waits for them, and re-layouts  3.08 us

profile of v2, /device:TPU:33, one launch (start us, length us, event | category | flops | bytes accessed | tf_op | source)
XLA Modules:
  0.0 137.9 jit_solution(5203787282777086744)
XLA Ops:
  0.6 134.2 %joint_attention.1 = (bf16[64,3072]{1,0:T(8,128)(2,1)}, bf16[2,3072]{1,0:T(2,128)(2,1)}) custom-call(bf16[3,64,3072]{2,1,0:T(8,128)(2,1)} %vid.1, bf16[3,2,3072]{2,1,0:T(2,128)(2,1)} %txt.1, f32[24,128]{1,0:T(8,128)} %bitcast.2, f32[24,128]{1,0:T(8,128)} %bitcast.3), custom_call_target="tpu_custom_call" | custom-call | tf_op jit(solution)/shard_map/joint_attention/pallas_call | solution.py:300
  134.8 1.8 %copy.8 = bf16[64,3072]{1,0:T(8,128)(2,1)} copy(bf16[64,3072]{1,0:T(8,128)(2,1)} %get-tuple-element.4) | data formatting | bytes 786432
  136.6 1.3 copy.9

commit v3 on v2

--- a/solution.py
+++ b/solution.py
@@ -12,6 +12,7 @@
 MESH = pl.DeviceIdType.MESH
 TILES = 3
 LAG = 3
+DEPTH = 2 * LAG + 2
 
 
 def near(j, n):
@@ -23,7 +24,7 @@
 def kernel(
     nb, nu, vid, txt, vgate, tgate, vout, tout,
     st, stt, kvb, txb, qb, qtb, ob, otb, qf, qq, ktx, tf, m_sc, acc_sc, s_a, s_b,
-    l_st, l_kv, l_q, zs_kv, zr_kv, zs_t, zr_t, zs_q, zr_q, zs_qt, zr_qt,
+    l_st, l_kv, l_q, zs_kv, zs_r, zr_kv, zs_t, zr_t, zs_q, zr_q, zs_qt, zr_qt,
     xs, xl, xr, xf0, xf1, pc, ts, tr, os_, orv, ots, otr, ol,
 ):
     z = lax.axis_index("blk")
@@ -76,12 +77,12 @@
         return lax.rem(z + nb + (2 * par - 1) * e, nb)
 
     hs = low(z)
-    for k in range(2):
+    for k, h in enumerate((own(z), shared(z))):
         pltpu.make_async_copy(
-            vid.at[pl.ds(1, 2), :, cols(hs + k)], kvb.at[u, 0, k], l_kv.at[k]
+            vid.at[pl.ds(1, 2), :, cols(h)], kvb.at[k, u, 0], zr_kv.at[k, 0]
         ).start()
         pltpu.make_async_copy(
-            txt.at[pl.ds(1, 2), :, cols(hs + k)], txb.at[u, 0, k], l_kv.at[2 + k]
+            txt.at[pl.ds(1, 2), :, cols(hs + k)], txb.at[u, 0, k], l_kv.at[k]
         ).start()
     for k, (s, h) in enumerate(((1, own(z)), (2, shared(z)))):
         pltpu.make_async_copy(vid.at[0, :, cols(h)], qb.at[s, per - 1], l_q.at[2 * k]).start()
@@ -96,7 +97,7 @@
             src_ref=src, dst_ref=dst, send_sem=ss, recv_sem=rs, device_id=dev, device_id_type=MESH
         ).start()
 
-    for s in range(TILES):
+    def send_queries(s):
         for i in range(per):
             if s < 2:
                 d = near(nb - 1 - per * s - i, nb)
@@ -109,45 +110,64 @@
             if d != 0:
                 send(st.at[h, 0], qb.at[s, i], zs_q, zr_q.at[s], {"blk": t})
                 send(stt.at[h, 0], qtb.at[s, i], zs_qt, zr_qt.at[s], {"blk": t})
+
+    def send_own(j):
+        d = near(j, nb)
+        t = lax.rem(z + nb - d, nb)
+        send(st.at[own(t), pl.ds(1, 2)], kvb.at[0, u, d], zs_kv, zr_kv.at[0, d], {"blk": t})
+
+    send_queries(0)
+    send_queries(1)
     for j in range(1, nb):
         d = near(j, nb)
         t = lax.rem(z + nb - d, nb)
         h = low(t)
         send(stt.at[pl.ds(h, 2), pl.ds(1, 2)], txb.at[u, d], zs_t, zr_t, {"blk": t})
-    for j in range(1, nb):
-        d = near(j, nb)
-        t = lax.rem(z + nb - d, nb)
-        h = low(t)
-        send(st.at[pl.ds(h, 2), pl.ds(1, 2)], kvb.at[u, d], zs_kv, zr_kv.at[d], {"blk": t})
+    for e in range(1, per):
+        t = shared_to(e)
+        send(st.at[shared(t), pl.ds(1, 2)], kvb.at[1, u, e], zs_kv, zr_kv.at[1, e], {"blk": t})
+    for j in range(1, per + 1):
+        send_own(j)
+
+    def piece_of(q):
+        r = q - 2 * per
+        late = lax.rem(r + 2 * per, 2)
+        slot = jnp.where(q < per, 1, jnp.where(q < 2 * per, 0, late))
+        j = jnp.where(q < 2 * per, q - per, per + r // 2)
+        idx = jnp.where(q < per, q, jnp.where(late * (r >= 0) == 1, per + r // 2, near(jnp.maximum(j, 0), nb)))
+        return slot, idx
 
     def arrived(ref, sem):
         pltpu.make_async_copy(ref, ref, sem).wait()
 
     right, left, partner = {"uly": ur}, {"uly": ul}, {"uly": up}
 
-    def pass_own(d):
-        piece = kvb.at[u, d]
-        send(piece, piece, xs.at[0], xl.at[d], right)
-        send(piece, piece, xs.at[1], xr.at[d], left)
-        send(piece, piece, xs.at[2], pc.at[d], partner)
-
-    def own_piece(d):
-        arrived(kvb.at[u, d], zr_kv.at[d])
-        pass_own(d)
-
-    def next_piece(d):
-        arrived(kvb.at[ul, d], xl.at[d])
-        send(kvb.at[ul, d, 0], kvb.at[ul, d, 0], xs.at[0], xf0.at[d], right)
-        send(kvb.at[ul, d], kvb.at[ul, d], xs.at[2], pc.at[d], partner)
-        arrived(kvb.at[ur, d], xr.at[d])
-        send(kvb.at[ur, d, 1], kvb.at[ur, d, 1], xs.at[1], xf1.at[d], left)
-        send(kvb.at[ur, d], kvb.at[ur, d], xs.at[2], pc.at[d], partner)
-
-    def far_piece(d):
-        arrived(kvb.at[uf, d, 0], xf0.at[d])
-        send(kvb.at[uf, d, 0], kvb.at[uf, d, 0], xs.at[2], pc.at[d], partner)
-        arrived(kvb.at[uf, d, 1], xf1.at[d])
-        send(kvb.at[uf, d, 1], kvb.at[uf, d, 1], xs.at[2], pc.at[d], partner)
+    def own_piece(q):
+        k, i = piece_of(q)
+        piece = kvb.at[k, u, i]
+        arrived(piece, zr_kv.at[k, i])
+        send(piece, piece, xs.at[0], xl.at[k, i], right)
+        send(piece, piece, xs.at[1], xr.at[k, i], left)
+        send(piece, piece, xs.at[2], pc.at[k, i], partner)
+
+    def hand_on(e):
+        send(kvb.at[1, u, e], kvb.at[1, u, per + e], zs_r, zr_kv.at[1, per + e], {"blk": z + 1 - 2 * par})
+
+    def next_piece(q):
+        k, i = piece_of(q)
+        arrived(kvb.at[k, ul, i], xl.at[k, i])
+        send(kvb.at[k, ul, i, 0], kvb.at[k, ul, i, 0], xs.at[0], xf0.at[k, i], right)
+        send(kvb.at[k, ul, i], kvb.at[k, ul, i], xs.at[2], pc.at[k, i], partner)
+        arrived(kvb.at[k, ur, i], xr.at[k, i])
+        send(kvb.at[k, ur, i, 1], kvb.at[k, ur, i, 1], xs.at[1], xf1.at[k, i], left)
+        send(kvb.at[k, ur, i], kvb.at[k, ur, i], xs.at[2], pc.at[k, i], partner)
+
+    def far_piece(q):
+        k, i = piece_of(q)
+        arrived(kvb.at[k, uf, i, 0], xf0.at[k, i])
+        send(kvb.at[k, uf, i, 0], kvb.at[k, uf, i, 0], xs.at[2], pc.at[k, i], partner)
+        arrived(kvb.at[k, uf, i, 1], xf1.at[k, i])
+        send(kvb.at[k, uf, i, 1], kvb.at[k, uf, i, 1], xs.at[2], pc.at[k, i], partner)
 
     scale = math.log2(math.e) / math.sqrt(HD)
     vrows = per * rows
@@ -172,30 +192,16 @@
         acc_sc[s, :, :HD] = acc_sc[s, :, :HD] * factor + product[:, :HD]
         acc_sc[s, :, HD:] = acc_sc[s, :, HD:] * factor + product[:, HD:]
 
+    bufs = (s_a, s_b)
+
     def step(block, n):
-        bufs = (s_a, s_b)
-        for s in range(TILES + 1):
-            if s < TILES:
+        for s in range(3):
+            if s < 2:
                 bufs[s % 2][:, :n] = scores_of(s, block(slots[s], 0))
             if s > 0:
                 soften(s - 1, bufs[(s - 1) % 2].at[:, :n], block(slots[s - 1], 1))
 
-    for k in range(2):
-        arrived(kvb.at[u, 0, k], l_kv.at[k])
-    pass_own(0)
-    for j in range(1, LAG):
-        own_piece(near(j, nb))
-        next_piece(near(j - 1, nb))
-        if j >= 2:
-            far_piece(near(j - 2, nb))
-
-    for k in range(2):
-        arrived(txb.at[u, 0, k], l_kv.at[2 + k])
-    arrived(txb.at[u, pl.ds(1, nb - 1)], zr_t)
-    for e in range(1, nu):
-        send(txb.at[u], txb.at[u], ts, tr, {"uly": lax.rem(u + e, nu)})
-
-    for s in range(TILES):
+    def prepare(s):
         remote = per
         if s > 0:
             arrived(qb.at[s, per - 1], l_q.at[2 * (s - 1)])
@@ -211,40 +217,8 @@
         high = scaled.astype(jnp.bfloat16)
         qq[s, :, :HD] = high
         qq[s, :, HD:] = (scaled - high.astype(jnp.float32)).astype(jnp.bfloat16)
-    m_sc[...] = jnp.full(m_sc.shape, -jnp.inf, jnp.float32)
-    acc_sc[...] = jnp.zeros(acc_sc.shape, jnp.float32)
-
-    arrived(txb.at[pl.ds(0, nu - 1)], tr)
-    for k in range(2):
-        for kv in range(2):
-            for v in range(nu):
-                for d in range(nb):
-                    at = (v * nb + d) * trows
-                    tf[at : at + trows, :] = txb[v, d, k, kv].astype(jnp.float32)
-            ktx[k, kv] = tf[...].astype(jnp.bfloat16)
-    step(lambda slot, kv: ktx[slot, kv], nu * nb * trows)
-
-    def turn(j, _):
-        @pl.when(j < nb)
-        def _():
-            own_piece(near(j, nb))
-
-        @pl.when(j < nb + 1)
-        def _():
-            next_piece(near(j - 1, nb))
-
-        @pl.when(j < nb + 2)
-        def _():
-            far_piece(near(j - 2, nb))
-
-        d = near(j - LAG, nb)
-        arrived(kvb.at[pl.ds(0, nu // 2), 0], pc.at[d])
-        step(lambda slot, kv: kvb[:, d, slot, kv].reshape(nu * rows, HD), nu * rows)
-        return 0
-
-    lax.fori_loop(LAG, nb + LAG, turn, 0)
-
-    for s in range(TILES):
+
+    def finish(s):
         h = own(z) if s < 2 else shared(z)
         attended = (acc_sc[s, :, :HD] / acc_sc[s, :, HD:]).astype(jnp.bfloat16).astype(jnp.float32)
         gated = attended[:vrows] * vgate[pl.ds(h, 1), :]
@@ -267,21 +241,117 @@
                 send(ob.at[s, i], vout.at[:, cols(h)], os_, orv, {"blk": t})
                 send(otb.at[s, i], tout.at[:, cols(h)], ots, otr, {"blk": t})
 
+    def carry(q):
+        @pl.when(q < 2 * nb)
+        def _():
+            own_piece(q)
+
+        @pl.when(q < per)
+        def _():
+            hand_on(q)
+
+        @pl.when((q >= 1) & (q < per))
+        def _():
+            send_own(per + q)
+
+        @pl.when((q >= LAG) & (q < 2 * nb + LAG))
+        def _():
+            next_piece(q - LAG)
+
+        @pl.when((q >= 2 * LAG) & (q < 2 * nb + 2 * LAG))
+        def _():
+            far_piece(q - 2 * LAG)
+
+    def early(q, _):
+        carry(q)
+        return 0
+
+    lax.fori_loop(0, per, early, 0)
+    send_queries(2)
+
+    for k in range(2):
+        arrived(txb.at[u, 0, k], l_kv.at[k])
+    arrived(txb.at[u, pl.ds(1, nb - 1)], zr_t)
+    for e in range(1, nu):
+        send(txb.at[u], txb.at[u], ts, tr, {"uly": lax.rem(u + e, nu)})
+    m_sc[...] = jnp.full(m_sc.shape, -jnp.inf, jnp.float32)
+    acc_sc[...] = jnp.zeros(acc_sc.shape, jnp.float32)
+    prepare(0)
+    prepare(1)
+    lax.fori_loop(per, per + LAG, early, 0)
+
+    arrived(txb.at[pl.ds(0, nu - 1)], tr)
+    for k in range(2):
+        for kv in range(2):
+            for v in range(nu):
+                for d in range(nb):
+                    at = (v * nb + d) * trows
+                    tf[at : at + trows, :] = txb[v, d, k, kv].astype(jnp.float32)
+            ktx[k, kv] = tf[...].astype(jnp.bfloat16)
+    step(lambda slot, kv: ktx[slot, kv], nu * nb * trows)
+
+    quarter = kvb.at[0, pl.ds(0, nu // 2), 0]
+
+    def turn(q, _):
+        carry(q)
+        r = q - DEPTH
+
+        @pl.when((r >= per) & ((r < 2 * per) | (lax.rem(r + DEPTH, 2) == 0)))
+        def _():
+            k, d = piece_of(r)
+            arrived(quarter, pc.at[0, d])
+            step(lambda slot, kv: kvb[0, :, d, kv].reshape(nu * rows, HD), nu * rows)
+
+        return 0
+
+    lax.fori_loop(per + LAG, 2 * nb + DEPTH - 1, turn, 0)
+    finish(0)
+    finish(1)
+
+    prepare(2)
+    n = nu * nb * trows
+
+    def shared_block(b, kv):
+        return kvb[1, :, b, kv].reshape(nu * rows, HD)
+
+    arrived(quarter, pc.at[1, 0])
+    s_a[...] = scores_of(2, shared_block(0, 0))
+
+    def pair(i, _):
+        b = 2 * i
+        arrived(quarter, pc.at[1, b + 1])
+        s_b[...] = scores_of(2, shared_block(b + 1, 0))
+        soften(2, s_a, shared_block(b, 1))
+
+        @pl.when(b + 2 < nb)
+        def _():
+            arrived(quarter, pc.at[1, b + 2])
+
+        s_a[...] = scores_of(2, shared_block(lax.rem(b + 2, nb), 0))
+        soften(2, s_b, shared_block(b + 1, 1))
+        return 0
+
+    lax.fori_loop(0, per, pair, 0)
+    s_b[:, :n] = scores_of(2, ktx[slots[2], 0])
+    soften(2, s_b.at[:, :n], ktx[slots[2], 1])
+    finish(2)
+
     for k in range(2):
         arrived(ob.at[0, 0], ol.at[2 * k])
         arrived(otb.at[0, 0], ol.at[2 * k + 1])
     n_out = nb - 1 + per - 1
-    some = kvb.at[0, pl.ds(0, n_out // 2), 0]
+    some = kvb.at[0, 0, pl.ds(0, n_out // 2)]
     small = txb.at[0, pl.ds(0, n_out // 2), 0]
     for sem in (os_, orv, zs_q):
         arrived(some, sem)
     for sem in (ots, otr, zs_qt):
         arrived(small, sem)
-    arrived(kvb.at[0, pl.ds(0, nb - 1)], zs_kv)
+    arrived(kvb.at[0, pl.ds(0, 2), pl.ds(0, n_out // 2)], zs_kv)
+    arrived(kvb.at[0, 0, pl.ds(0, per)], zs_r)
     arrived(txb.at[0, pl.ds(0, nb - 1)], zs_t)
-    arrived(kvb.at[pl.ds(0, 3), pl.ds(0, nb // 2)], xs.at[0])
-    arrived(kvb.at[pl.ds(0, 3), pl.ds(0, nb // 2)], xs.at[1])
-    arrived(kvb.at[pl.ds(0, nu // 2)], xs.at[2])
+    arrived(kvb.at[0, pl.ds(0, 3)], xs.at[0])
+    arrived(kvb.at[0, pl.ds(0, 3)], xs.at[1])
+    arrived(kvb.at[0], xs.at[2])
     arrived(txb.at[pl.ds(0, nu - 1)], ts)
 
 
@@ -308,7 +378,7 @@
         scratch_shapes=[
             pltpu.VMEM((heads, 3, rows, HD), bf),
             pltpu.VMEM((heads, 3, trows, HD), bf),
-            pltpu.VMEM((nu, nb, 2, 2, rows, HD), bf),
+            pltpu.VMEM((2, nu, nb, 2, rows, HD), bf),
             pltpu.VMEM((nu, nb, 2, 2, trows, HD), bf),
             pltpu.VMEM((TILES, per, rows, HD), bf),
             pltpu.VMEM((TILES, per, trows, HD), bf),
@@ -322,9 +392,9 @@
             pltpu.VMEM((TILES, tile, 2 * HD), f32),
             pltpu.VMEM((tile, nu * rows), f32),
             pltpu.VMEM((tile, nu * rows), f32),
-            dma((2,)), dma((4,)), dma((4,)),
-            dma(()), dma((nb,)), dma(()), dma(()), dma(()), dma((TILES,)), dma(()), dma((TILES,)),
-            dma((3,)), dma((nb,)), dma((nb,)), dma((nb,)), dma((nb,)), dma((nb,)),
+            dma((2,)), dma((2,)), dma((4,)),
+            dma(()), dma(()), dma((2, nb)), dma(()), dma(()), dma(()), dma((TILES,)), dma(()), dma((TILES,)),
+            dma((3,)), dma((2, nb)), dma((2, nb)), dma((2, nb)), dma((2, nb)), dma((2, nb)),
             dma(()), dma(()),
             dma(()), dma(()), dma(()), dma(()), dma((4,)),
         ],

time: 138 us -> 129 us (0.935)
  Pallas kernels: 134 us -> 125 us
    pallas_call x1, Pallas kernels: 134 us -> 125 us  [on_device(): pl.pallas_call(functools.partial(kernel, nb, nu), out_shape=(jax.ShapeDty...]
where the time goes in v3:
time: 129 us
  Pallas kernels  125 us (97%)
  local copies, waits for them, and re-layouts  3.08 us (2%)
    pallas_call x1, Pallas kernels, on_device(): pl.pallas_call(functools.partial(kernel, nb, nu), out_shape=(jax.ShapeDty...  125 us
    unnamed x2, local copies, waits for them, and re-layouts  3.08 us

profile of v3, /device:TPU:33, one launch (start us, length us, event | category | flops | bytes accessed | tf_op | source)
XLA Modules:
  0.0 129.2 jit_solution(18006222622216391198)
XLA Ops:
  0.6 125.5 %joint_attention.1 = (bf16[64,3072]{1,0:T(8,128)(2,1)}, bf16[2,3072]{1,0:T(2,128)(2,1)}) custom-call(bf16[3,64,3072]{2,1,0:T(8,128)(2,1)} %vid.1, bf16[3,2,3072]{2,1,0:T(2,128)(2,1)} %txt.1, f32[24,128]{1,0:T(8,128)} %bitcast.2, f32[24,128]{1,0:T(8,128)} %bitcast.3), custom_call_target="tpu_custom_call" | custom-call | tf_op jit(solution)/shard_map/joint_attention/pallas_call | solution.py:370
  126.1 1.8 %copy.8 = bf16[64,3072]{1,0:T(8,128)(2,1)} copy(bf16[64,3072]{1,0:T(8,128)(2,1)} %get-tuple-element.4) | data formatting | bytes 786432
  127.9 1.3 %copy.9 = bf16[2,3072]{1,0:T(2,128)(2,1)} copy(bf16[2,3072]{1,0:T(2,128)(2,1)} %get-tuple-element.5) | data formatting | bytes 24576

commit v4 on v3

--- a/solution.py
+++ b/solution.py
@@ -114,7 +114,7 @@
     def send_own(j):
         d = near(j, nb)
         t = lax.rem(z + nb - d, nb)
-        send(st.at[own(t), pl.ds(1, 2)], kvb.at[0, u, d], zs_kv, zr_kv.at[0, d], {"blk": t})
+        send(st.at[own(t), pl.ds(1, 2)], kvb.at[0, u, j], zs_kv, zr_kv.at[0, j], {"blk": t})
 
     send_queries(0)
     send_queries(1)
@@ -130,11 +130,9 @@
         send_own(j)
 
     def piece_of(q):
-        r = q - 2 * per
-        late = lax.rem(r + 2 * per, 2)
+        late = lax.rem(q, 2)
         slot = jnp.where(q < per, 1, jnp.where(q < 2 * per, 0, late))
-        j = jnp.where(q < 2 * per, q - per, per + r // 2)
-        idx = jnp.where(q < per, q, jnp.where(late * (r >= 0) == 1, per + r // 2, near(jnp.maximum(j, 0), nb)))
+        idx = jnp.where(q < per, q, jnp.where(q < 2 * per, q - per, q // 2))
         return slot, idx
 
     def arrived(ref, sem):
@@ -291,16 +289,36 @@
     step(lambda slot, kv: ktx[slot, kv], nu * nb * trows)
 
     quarter = kvb.at[0, pl.ds(0, nu // 2), 0]
+    wide = 2 * nu * rows
+
+    def keys_in(k, p):
+        arrived(quarter, pc.at[k, 2 * p])
+        arrived(quarter, pc.at[k, 2 * p + 1])
+
+    def block(k, p, kv):
+        return kvb[k, :, pl.ds(2 * p, 2), kv].reshape(wide, HD)
 
     def turn(q, _):
         carry(q)
         r = q - DEPTH
-
-        @pl.when((r >= per) & ((r < 2 * per) | (lax.rem(r + DEPTH, 2) == 0)))
-        def _():
-            k, d = piece_of(r)
-            arrived(quarter, pc.at[0, d])
-            step(lambda slot, kv: kvb[0, :, d, kv].reshape(nu * rows, HD), nu * rows)
+        place = lax.rem(r, 4)
+
+        @pl.when(r == 2 * per)
+        def _():
+            prepare(2)
+
+        @pl.when(((r > per) & (r < 2 * per) & (lax.rem(r, 2) == 1)) | ((r > 2 * per) & (place == 2)))
+        def _():
+            p = jnp.where(r < 2 * per, (r - per) // 2, r // 4)
+            keys_in(0, p)
+            step(lambda slot, kv: block(0, p, kv), wide)
+
+        @pl.when((r >= 2 * per) & (place == 0))
+        def _():
+            p = r // 4 - per // 2
+            keys_in(1, p)
+            s_a[...] = scores_of(2, block(1, p, 0))
+            soften(2, s_a, block(1, p, 1))
 
         return 0
 
@@ -308,32 +326,17 @@
     finish(0)
     finish(1)
 
-    prepare(2)
     n = nu * nb * trows
-
-    def shared_block(b, kv):
-        return kvb[1, :, b, kv].reshape(nu * rows, HD)
-
-    arrived(quarter, pc.at[1, 0])
-    s_a[...] = scores_of(2, shared_block(0, 0))
-
-    def pair(i, _):
-        b = 2 * i
-        arrived(quarter, pc.at[1, b + 1])
-        s_b[...] = scores_of(2, shared_block(b + 1, 0))
-        soften(2, s_a, shared_block(b, 1))
-
-        @pl.when(b + 2 < nb)
-        def _():
-            arrived(quarter, pc.at[1, b + 2])
-
-        s_a[...] = scores_of(2, shared_block(lax.rem(b + 2, nb), 0))
-        soften(2, s_b, shared_block(b + 1, 1))
-        return 0
-
-    lax.fori_loop(0, per, pair, 0)
-    s_b[:, :n] = scores_of(2, ktx[slots[2], 0])
-    soften(2, s_b.at[:, :n], ktx[slots[2], 1])
+    bufs[0][:, :n] = scores_of(2, ktx[slots[2], 0])
+    for i in range(per // 2):
+        p = per // 2 + i
+        keys_in(1, p)
+        bufs[(i + 1) % 2][...] = scores_of(2, block(1, p, 0))
+        if i == 0:
+            soften(2, bufs[0].at[:, :n], ktx[slots[2], 1])
+        else:
+            soften(2, bufs[i % 2], block(1, p - 1, 1))
+    soften(2, bufs[(per // 2) % 2], block(1, per - 1, 1))
     finish(2)
 
     for k in range(2):
@@ -390,8 +393,8 @@
             pltpu.VMEM((nu * nb * trows, HD), f32),
             pltpu.VMEM((TILES, tile, HD), f32),
             pltpu.VMEM((TILES, tile, 2 * HD), f32),
-            pltpu.VMEM((tile, nu * rows), f32),
-            pltpu.VMEM((tile, nu * rows), f32),
+            pltpu.VMEM((tile, 2 * nu * rows), f32),
+            pltpu.VMEM((tile, 2 * nu * rows), f32),
             dma((2,)), dma((2,)), dma((4,)),
             dma(()), dma(()), dma((2, nb)), dma(()), dma(()), dma(()), dma((TILES,)), dma(()), dma((TILES,)),
             dma((3,)), dma((2, nb)), dma((2, nb)), dma((2, nb)), dma((2, nb)), dma((2, nb)),

time: 129 us -> 130 us (level)
  no operation moved by 1% of the time
where the time goes in v4:
time: 130 us; the launch traced here: 129 us
  Pallas kernels  125 us (96%)
  local copies, waits for them, and re-layouts  3.08 us (2%)
    pallas_call x1, Pallas kernels, on_device(): pl.pallas_call(functools.partial(kernel, nb, nu), out_shape=(jax.ShapeDty...  125 us
    unnamed x2, local copies, waits for them, and re-layouts  3.08 us

profile of v4, /device:TPU:33, one launch (start us, length us, event | category | flops | bytes accessed | tf_op | source)
XLA Modules:
  0.0 129.2 jit_solution(16077576155665255856)
XLA Ops:
  0.6 125.5 %joint_attention.1 = (bf16[64,3072]{1,0:T(8,128)(2,1)}, bf16[2,3072]{1,0:T(2,128)(2,1)}) custom-call(bf16[3,64,3072]{2,1,0:T(8,128)(2,1)} %vid.1, bf16[3,2,3072]{2,1,0:T(2,128)(2,1)} %txt.1, f32[24,128]{1,0:T(8,128)} %bitcast.2, f32[24,128]{1,0:T(8,128)} %bitcast.3), custom_call_target="tpu_custom_call" | custom-call | tf_op jit(solution)/shard_map/joint_attention/pallas_call | solution.py:373
  126.1 1.8 %copy.8 = bf16[64,3072]{1,0:T(8,128)(2,1)} copy(bf16[64,3072]{1,0:T(8,128)(2,1)} %get-tuple-element.4) | data formatting | bytes 786432
  127.9 1.3 %copy.9 = bf16[2,3072]{1,0:T(2,128)(2,1)} copy(bf16[2,3072]{1,0:T(2,128)(2,1)} %get-tuple-element.5) | data formatting | bytes 24576

commit v5 on v4

--- a/solution.py
+++ b/solution.py
@@ -11,7 +11,7 @@
 HD = 128
 MESH = pl.DeviceIdType.MESH
 TILES = 3
-LAG = 3
+LAG = 4
 DEPTH = 2 * LAG + 2
 
 

time: 130 us -> 126 us (0.969)
  Pallas kernels: 125 us -> 122 us
    pallas_call x1, Pallas kernels: 125 us -> 122 us  [on_device(): pl.pallas_call(functools.partial(kernel, nb, nu), out_shape=(jax.ShapeDty...]
where the time goes in v5:
time: 126 us
  Pallas kernels  122 us (97%)
  local copies, waits for them, and re-layouts  3.08 us (2%)
    pallas_call x1, Pallas kernels, on_device(): pl.pallas_call(functools.partial(kernel, nb, nu), out_shape=(jax.ShapeDty...  122 us
    unnamed x2, local copies, waits for them, and re-layouts  3.08 us

profile of v5, /device:TPU:33, one launch (start us, length us, event | category | flops | bytes accessed | tf_op | source)
XLA Modules:
  0.0 126.0 jit_solution(8558934382518034761)
XLA Ops:
  0.6 122.3 %joint_attention.1 = (bf16[64,3072]{1,0:T(8,128)(2,1)}, bf16[2,3072]{1,0:T(2,128)(2,1)}) custom-call(bf16[3,64,3072]{2,1,0:T(8,128)(2,1)} %vid.1, bf16[3,2,3072]{2,1,0:T(2,128)(2,1)} %txt.1, f32[24,128]{1,0:T(8,128)} %bitcast.2, f32[24,128]{1,0:T(8,128)} %bitcast.3), custom_call_target="tpu_custom_call" | custom-call | tf_op jit(solution)/shard_map/joint_attention/pallas_call | solution.py:373
  122.9 1.8 %copy.8 = bf16[64,3072]{1,0:T(8,128)(2,1)} copy(bf16[64,3072]{1,0:T(8,128)(2,1)} %get-tuple-element.4) | data formatting | bytes 786432
  124.7 1.3 %copy.9 = bf16[2,3072]{1,0:T(2,128)(2,1)} copy(bf16[2,3072]{1,0:T(2,128)(2,1)} %get-tuple-element.5) | data formatting | bytes 24576
